TPU v7x, 32 devices: a whole 2x2x4 slice. The times are simulated.
32 devices in a mesh: dp: 8 (over z, x), tensor: 4 (over y, core).
Axes of the slice: x: 2, y: 2, z: 4, core: 2. Of those that a mesh axis runs over, the one named last changes fastest.
Arguments:
- attn_out: bfloat16 [4096, 2560], P('dp', 'tensor'), may hold values from -6 to 6
- resid: bfloat16 [4096, 5120], P('dp', 'tensor'), may hold values from -6 to 6
- out_proj: bfloat16 [2560, 5120], P('tensor'), may hold values from -0.125 to 0.125
- heads: bfloat16 [5120, 8], P('tensor'), may hold values from -0.078125 to 0.078125
- gain: bfloat16 [5120], P('tensor'), may hold values from 0.25 to 1.75
- lengths: int32 [64], P('dp'), may hold values from 0 to 63
Outputs:
- uwo: float32 [64], P('dp')
- proj_grad: float32 [5120, 2560], P('dp', 'tensor')
- head_grad: float32 [5120, 8], P('tensor')
- gain_grad: float32 [5120], P('tensor')
Inputs may be any that keep to these rules, and one draw needn't show every extreme that they name: Positions 0 to lengths[n] of response n are scored.
All inputs are finite; a program needn't handle non-finite values.
Results may differ from a plain program's by a relative error of at most 0.0085.
Values may be sent and summed in bfloat16 or wider, within the bound.
A program may use at most 128 MiB of HBM per device.

v0:
```python
import jax
import jax.numpy as jnp
from jax import lax
from jax.sharding import PartitionSpec as P

D = 5120
EPS_NORM = 1e-06
EPS_VAR = 1e-05
PENALTY = 0.5


def per_device(attn_out, resid, out_proj, heads, gain, lengths):
    total_rows = attn_out.shape[0]
    resp_dev = lengths.shape[0]
    seq_len = total_rows // resp_dev
    members = heads.shape[1]
    highest = lax.Precision.HIGHEST
    product = jnp.dot(attn_out, out_proj, preferred_element_type=jnp.float32)
    gain_local = gain.astype(jnp.float32)
    heads_local = heads.astype(jnp.float32)
    hidden = resid.astype(jnp.float32) + lax.psum_scatter(
        product.astype(jnp.bfloat16), "tensor", scatter_dimension=1, tiled=True
    ).astype(jnp.float32)
    squares = lax.psum(jnp.sum(hidden * hidden, axis=1), "tensor")
    rinv = lax.rsqrt(squares / D + EPS_NORM)
    normed = hidden * rinv[:, None] * gain_local[None, :]
    scores = lax.psum(jnp.dot(normed, heads_local, precision=highest), "tensor")
    position = lax.broadcasted_iota(jnp.int32, (resp_dev, seq_len), 1)
    inside = position <= lengths[:, None]
    counts = (lengths + 1).astype(jnp.float32)
    per_resp = scores.reshape(resp_dev, seq_len, members)
    rewards = jnp.sum(jnp.where(inside[:, :, None], per_resp, 0.0), axis=1) / counts[:, None]
    total_resp = resp_dev * lax.axis_size("dp")
    first_sum, second_sum = lax.psum(
        (jnp.sum(rewards, axis=0), jnp.sum(rewards * rewards, axis=0)), "dp"
    )
    center = first_sum / total_resp
    spread = second_sum / total_resp - center * center
    zed = (rewards - center[None, :]) * lax.rsqrt(spread + EPS_VAR)[None, :]
    zmean = jnp.mean(zed, axis=1)
    uwo = zmean - PENALTY * jnp.mean((zed - zmean[:, None]) ** 2, axis=1)
    pairs = rewards.reshape(resp_dev // 2, 2, members)
    weight = jax.nn.sigmoid(pairs[:, 1] - pairs[:, 0])
    dreward = jnp.stack([-weight, weight], axis=1).reshape(resp_dev, members)
    dscore = jnp.where(inside[:, :, None], (dreward / counts[:, None])[:, None, :], 0.0).reshape(
        total_rows, members
    )
    dnormed_local = jnp.dot(dscore, heads_local.T, precision=highest)
    inner = lax.psum(jnp.sum(hidden * gain_local[None, :] * dnormed_local, axis=1), "tensor")
    dhidden = (
        rinv[:, None] * gain_local[None, :] * dnormed_local
        - hidden * (rinv**3 * inner / D)[:, None]
    ).astype(jnp.bfloat16)
    head_term = jnp.dot(normed.T, dscore, precision=highest)
    gain_term = jnp.sum(dnormed_local * hidden * rinv[:, None], axis=0)
    head_grad, gain_grad = lax.psum((head_term, gain_term), "dp")
    term = jnp.einsum(
        "rd,rj->dj",
        lax.all_gather(dhidden, "tensor", axis=1, tiled=True),
        attn_out,
        preferred_element_type=jnp.float32,
    )
    proj_grad = lax.psum_scatter(term, "dp", scatter_dimension=0, tiled=True)
    return (uwo, proj_grad, head_grad, gain_grad)


def solution(mesh):
    return jax.shard_map(
        per_device,
        mesh=mesh,
        in_specs=(
            P("dp", "tensor"),
            P("dp", "tensor"),
            P("tensor", None),
            P("tensor", None),
            P("tensor"),
            P("dp"),
        ),
        out_specs=(P("dp"), P("dp", "tensor"), P("tensor", None), P("tensor")),
        check_vma=False,
    )
```

profile of v0, /device:TPU:0, one launch (start us, length us, event | category | flops | bytes accessed | tf_op | source)
XLA Modules:
  0.0 384.5 jit_solution(8206958620141189595)
XLA Ops:
  7.2 1.0 copy-done
  8.3 8.8 %convolution_convert_fusion = bf16[512,5120]{1,0:T(8,128)(2,1)} fusion(bf16[512,640]{1,0:T(8,128)(2,1)S(1)} %copy-done, bf16[640,5120]{1,0:T(8,128)(2,1)} %param.8), kind=kOutput, calls=%fused_computation | convolution fusion | flops 3358064640 | bytes 12451840 | tf_op jit(solution)/shard_map/dot_general | solution.py:18
  17.2 0.6 copy-done.8
  17.7 0.1 iota_compare_fusion
  17.8 0.6 le.18
  18.4 0.1 div.52
  18.5 0.1 copy.14
  18.6 52.6 %reduce-scatter.3.cloned.1.call-done = bf16[512,1280]{1,0:T(8,128)(2,1)} async-done(((bf16[512,5120]{1,0:T(8,128)(2,1)}), bf16[512,1280]{1,0:T(8,128)(2,1)}) %reduce-scatter.3.cloned.1.call-update) | async-done | bytes 1310736 | tf_op jit(solution)/shard_map/reduce_scatter | solution.py:21
  71.2 1.9 multiply_reduce_fusion.2
  73.1 5.8 %psum.49 = f32[512]{0:T(512)S(1)} all-reduce(f32[512]{0:T(512)S(1)} %multiply_reduce_fusion.2), channel_id=1, replica_groups=mesh['dp'=8,'tensor'=4] {'tensor'}, use_global_device_ids=true, to_apply=%region_2.0 | all-reduce | flops 512 | bytes 4096 | tf_op jit(solution)/shard_map/psum | solution.py:24
  78.9 1.7 fusion.1
  80.6 0.1 reshape.69
  80.7 10.3 %psum.50 = f32[8,64,8]{1,0,2:T(8,128)S(1)} all-reduce(f32[8,64,8]{1,0,2:T(8,128)S(1)} %reshape.69), channel_id=1, replica_groups=mesh['dp'=8,'tensor'=4] {'tensor'}, use_global_device_ids=true, to_apply=%region_3.0 | all-reduce | flops 4096 | bytes 32768 | tf_op jit(solution)/shard_map/psum | solution.py:27
  91.0 0.1 select_reduce_fusion
  91.1 0.1 copy_divide_fusion
  91.3 0.7 fusion.13
  92.0 0.7 copy.18
  92.7 0.8 bitcast_select_fusion
  93.5 4.6 %multiply_reduce_fusion = (f32[1280]{0:T(1024)}, f32[512]{0:T(512)}, f32[512,1280]{1,0:T(8,128)}) fusion(bf16[512,1280]{1,0:T(8,128)(2,1)S(1)} %copy-done.2, bf16[512,1280]{1,0:T(8,128)(2,1)S(1)} %copy-done.1, f32[512]{0:T(512)} %copy-done.3, f32[1280]{0:T(1024)S(1)} %convert_element_type.22, f32[512,8]{1,0:T(8,128)S(1)} %bitcast_select_fusion, ...), kind=kOutput, calls=%fused_computation.1 | convolution fusion | flops 68811008 | bytes 5294080 | tf_op jit(solution)/shard_map/dot_general | solution.py:48
  98.2 6.8 %psum.53 = f32[512]{0:T(512)} all-reduce(f32[512]{0:T(512)} %get-tuple-element.5), channel_id=1, replica_groups=mesh['dp'=8,'tensor'=4] {'tensor'}, use_global_device_ids=true, to_apply=%region_12.13 | all-reduce | flops 512 | bytes 4096 | tf_op jit(solution)/shard_map/psum | solution.py:49
  105.0 0.7 fusion.8
  105.7 3.5 subtract_convert_fusion
  109.2 0.2 reduce-scatter.5.cloned.1.call-start
  109.5 40.8 %all-gather.2.cloned.1.call-done = bf16[512,5120]{1,0:T(8,128)(2,1)} async-done(((bf16[512,1280]{1,0:T(8,128)(2,1)}), bf16[512,5120]{1,0:T(8,128)(2,1)}) %all-gather.2.cloned.1.call-update) | async-done | bytes 5242896 | tf_op jit(solution)/shard_map/all_gather | solution.py:59
  150.2 11.4 %fusion.16 = f32[5120,640]{1,0:T(8,128)} fusion(bf16[512,5120]{1,0:T(8,128)(2,1)} %all-gather.2.cloned.1.call-done, bf16[512,640]{1,0:T(8,128)(2,1)S(1)} %copy-done), kind=kOutput, calls=%fused_computation.40 | convolution fusion | flops 3355443200 | bytes 19005440 | tf_op jit(solution)/shard_map/rd,rj->dj/dot_general | solution.py:57
  161.7 0.7 copy-done.4
  162.3 2.5 fusion
  164.9 41.5 %all-reduce = (f32[8]{0:T(128)S(1)}, f32[8]{0:T(128)S(1)}, f32[1280,8]{0,1:T(8,128)}, f32[1280]{0:T(1024)}) all-reduce(f32[8]{0:T(128)} %get-tuple-element.7, f32[8]{0:T(128)} %get-tuple-element.6, f32[1280,8]{0,1:T(8,128)} %fusion, f32[1280]{0:T(1024)} %get-tuple-element.4), channel_id=1, replica_groups=mesh['dp'=8,'tensor'=4] {'dp'}, use_global_device_ids=true, to_apply=%region_8.9 | all-reduce | flops 11536 | bytes 92288 | tf_op jit(solution)/shard_map/psum | solution.py:34
  206.4 0.8 fusion.6
  207.1 0.8 multiply_reduce_fusion.3
  207.9 0.5 multiply_subtract_fusion
  208.4 169.5 %reduce-scatter.5.cloned.1.call-done = f32[640,640]{1,0:T(8,128)} async-done(((f32[5120,640]{1,0:T(8,128)}), f32[640,640]{1,0:T(8,128)}) %reduce-scatter.5.cloned.1.call-update) | async-done | bytes 1638416 | tf_op jit(solution)/shard_map/reduce_scatter | solution.py:63
  (30 shorter events, 0.4 us)
Async XLA Ops:
  7.2 1.1 copy-start
  7.2 64.0 %reduce-scatter.3.cloned.1.call-start = ((), (), s32[]{:S(2)}) async-start(), calls=%async_computation.2 | async-start | bytes 6553600 | tf_op jit(solution)/shard_map/reduce_scatter | solution.py:21
  17.1 0.7 copy-start.8
  17.1 1.5 copy-start.6
  17.1 54.1 %copy-start.1 = (bf16[512,1280]{1,0:T(8,128)(2,1)S(1)}, bf16[512,1280]{1,0:T(8,128)(2,1)}, u32[]{:S(2)}) copy-start(bf16[512,1280]{1,0:T(8,128)(2,1)} %param.7) | copy-start | bytes 3932164
  17.1 61.8 %copy-start.7 = (bf16[1280,8]{0,1:T(8,128)(2,1)S(1)}, bf16[1280,8]{0,1:T(8,128)(2,1)}, u32[]{:S(2)}) copy-start(bf16[1280,8]{0,1:T(8,128)(2,1)} %param.9) | copy-start | bytes 61444
  17.1 133.1 %all-gather.2.cloned.1.call-start = ((), (), s32[]{:S(2)}) async-start(), calls=%async_computation.3 | async-start | bytes 6553600 | tf_op jit(solution)/shard_map/all_gather | solution.py:59
  18.4 72.9 %copy-start.5 = (f32[8]{0:T(128)}, f32[8]{0:T(128)S(1)}, u32[]{:S(2)}) copy-start(f32[8]{0:T(128)S(1)} %add_convert_fusion) | copy-start | bytes 100
  71.2 7.7 %copy-start.2 = (bf16[512,1280]{1,0:T(8,128)(2,1)S(1)}, bf16[512,1280]{1,0:T(8,128)(2,1)}, u32[]{:S(2)}) copy-start(bf16[512,1280]{1,0:T(8,128)(2,1)} %reduce-scatter.3.cloned.1.call-done) | copy-start | bytes 3932164
  78.9 1.8 copy-start.3
  109.2 268.7 %reduce-scatter.5.cloned.1.call-start = ((), (), s32[]{:S(2)}) async-start(), calls=%async_computation.4 | async-start | bytes 14745600 | tf_op jit(solution)/shard_map/reduce_scatter | solution.py:63
  161.7 0.7 copy-start.4
Sparse Core Ops, SparseCore 0:
  17.2 53.8 reduce-scatter.2
  109.4 40.8 all-gather.1
  161.8 216.0 reduce-scatter.4
where the time goes:
time: 385 us; the launch traced here: 384 us
  waiting for transfers between devices  263 us (68%)
  blocking collectives  64.3 us (17%)
  matrix products  29.2 us (8%)
  between operations  13.8 us (4%)
  other arithmetic  9.97 us (3%)
  local copies, waits for them, and re-layouts  3.95 us (1%)
    reduce_scatter x1, waiting for transfers between devices, per_device(): proj_grad = lax.psum_scatter(term, 'dp', scatter_dimension=0, tiled=True)  170 us
    reduce_scatter x1, waiting for transfers between devices, per_device(): lax.psum_scatter(product.astype(jnp.bfloat16), 'tensor', scatter_dimensio...  52.6 us
    psum x1, blocking collectives, per_device(): lax.psum((jnp.sum(rewards, axis=0), jnp.sum(rewards * rewards, axis=0)),...  41.5 us
    all_gather x1, waiting for transfers between devices, per_device(): lax.all_gather(dhidden, 'tensor', axis=1, tiled=True)  40.8 us
    dot_general x1, matrix products, per_device(): jnp.einsum('rd,rj->dj', lax.all_gather(dhidden, 'tensor', axis=1, tiled=T...  11.4 us
    psum x1, blocking collectives, per_device(): scores = lax.psum(jnp.dot(normed, heads_local, precision=highest), 'tensor')  10.3 us
    dot_general x1, matrix products, per_device(): product = jnp.dot(attn_out, out_proj, preferred_element_type=jnp.float32)  8.81 us
  transfers between devices with their start and end apart: 3, of which 3 were waited for; matrix products, arithmetic and copies ran while one was open for 1% of the time, Pallas kernels for 0%

commit v1 on v0

--- a/solution.py
+++ b/solution.py
@@ -56,7 +56,7 @@
     head_grad, gain_grad = lax.psum((head_term, gain_term), "dp")
     term = jnp.einsum(
         "rd,rj->dj",
-        lax.all_gather(dhidden, "tensor", axis=1, tiled=True),
+        jnp.concatenate(lax.all_gather(dhidden, "tensor"), axis=1),
         attn_out,
         preferred_element_type=jnp.float32,
     )

time: 385 us -> 393 us (1.021)
  local copies, waits for them, and re-layouts: 3.95 us -> 11.8 us
    all_gather x0 -> x1, local copies, waits for them, and re-layouts: none -> 7.86 us  [per_device(): lax.all_gather(dhidden, 'tensor')]
where the time goes in v1:
time: 393 us; the launch traced here: 392 us
  waiting for transfers between devices  263 us (67%)
  blocking collectives  64.3 us (16%)
  matrix products  29 us (7%)
  between operations  13.8 us (4%)
  local copies, waits for them, and re-layouts  11.8 us (3%)
  other arithmetic  9.92 us (3%)
    reduce_scatter x1, waiting for transfers between devices, per_device(): proj_grad = lax.psum_scatter(term, 'dp', scatter_dimension=0, tiled=True)  170 us
    reduce_scatter x1, waiting for transfers between devices, per_device(): lax.psum_scatter(product.astype(jnp.bfloat16), 'tensor', scatter_dimensio...  52.6 us
    psum x1, blocking collectives, per_device(): lax.psum((jnp.sum(rewards, axis=0), jnp.sum(rewards * rewards, axis=0)),...  41.5 us
    all_gather x1, waiting for transfers between devices, per_device(): lax.all_gather(dhidden, 'tensor')  40.8 us
    dot_general x1, matrix products, per_device(): jnp.einsum('rd,rj->dj', jnp.concatenate(lax.all_gather(dhidden, 'tensor')...  11.4 us
    psum x1, blocking collectives, per_device(): scores = lax.psum(jnp.dot(normed, heads_local, precision=highest), 'tensor')  10.3 us
    dot_general x1, matrix products, per_device(): product = jnp.dot(attn_out, out_proj, preferred_element_type=jnp.float32)  8.81 us
    all_gather x1, local copies, waits for them, and re-layouts, per_device(): lax.all_gather(dhidden, 'tensor')  7.86 us
  transfers between devices with their start and end apart: 3, of which 3 were waited for; matrix products, arithmetic and copies ran while one was open for 1% of the time, Pallas kernels for 0%

profile of v1, /device:TPU:0, one launch (start us, length us, event | category | flops | bytes accessed | tf_op | source)
XLA Modules:
  0.0 392.1 jit_solution(3511464624550125021)
XLA Ops:
  7.2 1.0 copy-done
  8.3 8.8 %convolution_convert_fusion = bf16[512,5120]{1,0:T(8,128)(2,1)} fusion(bf16[512,640]{1,0:T(8,128)(2,1)S(1)} %copy-done, bf16[640,5120]{1,0:T(8,128)(2,1)} %param.8), kind=kOutput, calls=%fused_computation | convolution fusion | flops 3358064640 | bytes 12451840 | tf_op jit(solution)/shard_map/dot_general | solution.py:18
  17.2 0.6 copy-done.8
  17.8 0.6 le.18
  18.4 0.1 div.52
  18.5 0.1 copy.16
  18.6 52.6 %reduce-scatter.3.cloned.1.call-done = bf16[512,1280]{1,0:T(8,128)(2,1)} async-done(((bf16[512,5120]{1,0:T(8,128)(2,1)}), bf16[512,1280]{1,0:T(8,128)(2,1)}) %reduce-scatter.3.cloned.1.call-update) | async-done | bytes 1310736 | tf_op jit(solution)/shard_map/reduce_scatter | solution.py:21
  71.2 1.9 multiply_reduce_fusion.2
  73.1 5.8 %psum.49 = f32[512]{0:T(512)S(1)} all-reduce(f32[512]{0:T(512)S(1)} %multiply_reduce_fusion.2), channel_id=1, replica_groups=mesh['dp'=8,'tensor'=4] {'tensor'}, use_global_device_ids=true, to_apply=%region_2.0 | all-reduce | flops 512 | bytes 4096 | tf_op jit(solution)/shard_map/psum | solution.py:24
  78.9 1.7 fusion.1
  80.6 0.1 reshape.75
  80.7 10.3 %psum.50 = f32[8,64,8]{1,0,2:T(8,128)S(1)} all-reduce(f32[8,64,8]{1,0,2:T(8,128)S(1)} %reshape.75), channel_id=1, replica_groups=mesh['dp'=8,'tensor'=4] {'tensor'}, use_global_device_ids=true, to_apply=%region_3.0 | all-reduce | flops 4096 | bytes 32768 | tf_op jit(solution)/shard_map/psum | solution.py:27
  90.9 0.1 select_reduce_fusion
  91.1 0.1 copy_divide_fusion
  91.3 0.7 fusion.13
  92.0 0.7 copy.20
  92.7 0.8 bitcast_select_fusion
  93.5 4.6 %multiply_reduce_fusion = (f32[1280]{0:T(1024)}, f32[512]{0:T(512)}, f32[512,1280]{1,0:T(8,128)}) fusion(bf16[512,1280]{1,0:T(8,128)(2,1)S(1)} %copy-done.2, bf16[512,1280]{1,0:T(8,128)(2,1)S(1)} %copy-done.1, f32[512]{0:T(512)} %copy-done.3, f32[1280]{0:T(1024)S(1)} %convert_element_type.22, f32[512,8]{1,0:T(8,128)S(1)} %bitcast_select_fusion, ...), kind=kOutput, calls=%fused_computation.1 | convolution fusion | flops 68811008 | bytes 5294080 | tf_op jit(solution)/shard_map/dot_general | solution.py:48
  98.1 6.8 %psum.53 = f32[512]{0:T(512)} all-reduce(f32[512]{0:T(512)} %get-tuple-element.5), channel_id=1, replica_groups=mesh['dp'=8,'tensor'=4] {'tensor'}, use_global_device_ids=true, to_apply=%region_12.13 | all-reduce | flops 512 | bytes 4096 | tf_op jit(solution)/shard_map/psum | solution.py:49
  104.9 0.7 fusion.8
  105.6 3.5 subtract_convert_fusion
  109.1 0.2 reduce-scatter.5.cloned.1.call-start
  109.3 40.8 %all-gather.3.cloned.1.call-done = bf16[2048,1280]{1,0:T(8,128)(2,1)} async-done(((bf16[512,1280]{1,0:T(8,128)(2,1)}), bf16[2048,1280]{1,0:T(8,128)(2,1)}) %all-gather.3.cloned.1.call-update) | async-done | bytes 5242896 | tf_op jit(solution)/shard_map/all_gather | solution.py:59
  150.1 7.9 %copy.21 = bf16[4,512,1280]{1,2,0:T(8,128)(2,1)} copy(bf16[4,512,1280]{2,1,0:T(8,128)(2,1)} %bitcast.19) | data formatting | bytes 10485760 | tf_op jit(solution)/shard_map/all_gather | solution.py:59
  158.0 11.4 %fusion.16 = f32[5120,640]{1,0:T(8,128)} fusion(bf16[512,5120]{0,1:T(8,128)(2,1)} %bitcast.18, bf16[512,640]{1,0:T(8,128)(2,1)S(1)} %copy-done), kind=kOutput, calls=%fused_computation.40 | convolution fusion | flops 3355443200 | bytes 19005440 | tf_op jit(solution)/shard_map/rd,rj->dj/dot_general | solution.py:57
  169.4 0.7 copy-done.4
  170.0 2.5 fusion
  172.6 41.5 %all-reduce = (f32[8]{0:T(128)S(1)}, f32[8]{0:T(128)S(1)}, f32[1280,8]{0,1:T(8,128)}, f32[1280]{0:T(1024)}) all-reduce(f32[8]{0:T(128)} %get-tuple-element.7, f32[8]{0:T(128)} %get-tuple-element.6, f32[1280,8]{0,1:T(8,128)} %fusion, f32[1280]{0:T(1024)} %get-tuple-element.4), channel_id=1, replica_groups=mesh['dp'=8,'tensor'=4] {'dp'}, use_global_device_ids=true, to_apply=%region_8.9 | all-reduce | flops 11536 | bytes 92288 | tf_op jit(solution)/shard_map/psum | solution.py:34
  214.0 0.8 fusion.6
  214.8 0.8 multiply_reduce_fusion.3
  215.6 0.5 multiply_subtract_fusion
  216.1 169.5 %reduce-scatter.5.cloned.1.call-done = f32[640,640]{1,0:T(8,128)} async-done(((f32[5120,640]{1,0:T(8,128)}), f32[640,640]{1,0:T(8,128)}) %reduce-scatter.5.cloned.1.call-update) | async-done | bytes 1638416 | tf_op jit(solution)/shard_map/reduce_scatter | solution.py:63
  (31 shorter events, 0.4 us)
Async XLA Ops:
  7.2 1.1 copy-start
  7.2 64.0 %reduce-scatter.3.cloned.1.call-start = ((), (), s32[]{:S(2)}) async-start(), calls=%async_computation.2 | async-start | bytes 6553600 | tf_op jit(solution)/shard_map/reduce_scatter | solution.py:21
  17.1 0.7 copy-start.8
  17.1 1.5 copy-start.6
  17.1 54.1 %copy-start.1 = (bf16[512,1280]{1,0:T(8,128)(2,1)S(1)}, bf16[512,1280]{1,0:T(8,128)(2,1)}, u32[]{:S(2)}) copy-start(bf16[512,1280]{1,0:T(8,128)(2,1)} %param.7) | copy-start | bytes 3932164
  17.1 61.8 %copy-start.7 = (bf16[1280,8]{0,1:T(8,128)(2,1)S(1)}, bf16[1280,8]{0,1:T(8,128)(2,1)}, u32[]{:S(2)}) copy-start(bf16[1280,8]{0,1:T(8,128)(2,1)} %param.9) | copy-start | bytes 61444
  17.1 133.0 %all-gather.3.cloned.1.call-start = ((), (), s32[]{:S(2)}) async-start(), calls=%async_computation.4 | async-start | bytes 6553600 | tf_op jit(solution)/shard_map/all_gather | solution.py:59
  18.4 72.9 %copy-start.5 = (f32[8]{0:T(128)}, f32[8]{0:T(128)S(1)}, u32[]{:S(2)}) copy-start(f32[8]{0:T(128)S(1)} %add_convert_fusion) | copy-start | bytes 100
  71.2 7.7 %copy-start.2 = (bf16[512,1280]{1,0:T(8,128)(2,1)S(1)}, bf16[512,1280]{1,0:T(8,128)(2,1)}, u32[]{:S(2)}) copy-start(bf16[512,1280]{1,0:T(8,128)(2,1)} %reduce-scatter.3.cloned.1.call-done) | copy-start | bytes 3932164
  78.9 1.7 copy-start.3
  109.1 276.5 %reduce-scatter.5.cloned.1.call-start = ((), (), s32[]{:S(2)}) async-start(), calls=%async_computation.3 | async-start | bytes 14745600 | tf_op jit(solution)/shard_map/reduce_scatter | solution.py:63
  169.4 0.7 copy-start.4
Sparse Core Ops, SparseCore 0:
  17.2 53.8 reduce-scatter.2
  109.2 40.8 all-gather.2
  169.5 216.0 reduce-scatter.4
